TPU v7x, 32 devices: a whole 2x2x4 slice. The times are simulated.
32 devices in a mesh: band: 4 (over y, x), ga: 8 (over z, core).
Axes of the slice: x: 2, y: 2, z: 4, core: 2. Of those that a mesh axis runs over, the one named last changes fastest.
Arguments:
- wavefunctions: bfloat16 [512, 98304], P('band', 'ga'), may hold values from -6 to 6
- projectors: bfloat16 [2048, 98304], P('band', 'ga'), may hold values from -0.125 to 0.125
- kinetic_diag: float32 [98304], P('ga'), may hold values from 0.1 to 4
- species_index: int32 [256], replicated, may hold values from 0 to 3
- coupling: float32 [4, 8, 8], replicated, may hold values from -5 to 5
Outputs:
- applied: bfloat16 [512, 98304], P('band', 'ga')
All inputs are finite; a program needn't handle non-finite values.
Results may differ from a plain program's by a relative error of at most 0.015.
Values may be sent and summed in bfloat16 or wider, within the bound.
A program may use at most 64 MiB of HBM per device.

v0:
```python
import functools

import jax
import jax.numpy as jnp
from jax import lax
from jax.experimental import pallas as pl
from jax.experimental.pallas import tpu as pltpu
from jax.sharding import PartitionSpec as P

CHUNKS = 2
TILES = 4
LANES = 128

NPA = 8


def apply_blocks(correlations, species_index, coupling, atom_start):
    rows = correlations.shape[0]
    count = correlations.shape[1] // NPA
    local_species = lax.dynamic_slice_in_dim(species_index, atom_start, count)
    onehot = (
        local_species[:, None] == jnp.arange(coupling.shape[0], dtype=jnp.int32)[None, :]
    ).astype(jnp.float32)
    blocks = jnp.einsum("as,sij->aij", onehot, coupling, precision=lax.Precision.HIGHEST)
    mixed = jnp.einsum(
        "baj,aij->bai",
        correlations.reshape(rows, count, NPA),
        blocks,
        precision=lax.Precision.HIGHEST,
    )
    return mixed.reshape(rows, count * NPA).astype(jnp.bfloat16)


def reduce_and_mix(partial_value, species_index, coupling, first_proj):
    total = lax.psum(partial_value.astype(jnp.bfloat16), "ga").astype(jnp.float32)
    return apply_blocks(total, species_index, coupling, first_proj // NPA)


def local(wavefunctions, projectors, kinetic_diag, species_index, coupling):
    proj_local = projectors.shape[0]
    band_index = lax.axis_index("band")
    partial_value = jnp.einsum(
        "bg,pg->bp",
        lax.all_gather(wavefunctions, "band", axis=0, tiled=True),
        projectors,
        preferred_element_type=jnp.float32,
    )
    mixed = reduce_and_mix(partial_value, species_index, coupling, band_index * proj_local)
    nonlocal_term = lax.psum_scatter(
        jnp.dot(mixed, projectors, preferred_element_type=jnp.float32).astype(jnp.bfloat16),
        "band",
        scatter_dimension=0,
        tiled=True,
    ).astype(jnp.float32)
    return (kinetic_diag[None, :] * wavefunctions.astype(jnp.float32) + nonlocal_term).astype(
        jnp.bfloat16
    )


def mixing_tiles(species_index, coupling, first_atom, count):
    npa = coupling.shape[1]
    local_species = lax.dynamic_slice_in_dim(species_index, first_atom, count)
    onehot = (
        local_species[:, None] == jnp.arange(coupling.shape[0], dtype=jnp.int32)[None, :]
    ).astype(jnp.float32)
    per_tile = LANES // npa
    spread = jnp.einsum("as,sij->jai", onehot, coupling, precision=lax.Precision.HIGHEST)
    spread = spread.reshape(npa, count // per_tile, LANES).transpose(1, 0, 2)
    spread = jnp.tile(spread, (1, per_tile, 1))
    atom_of = jnp.arange(LANES) // npa
    return jnp.where(atom_of[:, None] == atom_of[None, :], spread, 0.0)


def kernel(
    nga, wf, pj, tiles, out,
    proj, wave, acc, csend, crecv, sumf, sumb, parts, mine, theirs, nsend, nrecv, nfull,
    s_loc, s_p, s_wm, s_wo, s_wf, s_a, s_c, s_d, s_f, s_n, s_o,
):
    chunks, _, rows, half = wave.shape
    width = nsend.shape[-1]
    quarter = nga // 4
    band, me = lax.axis_index("band"), lax.axis_index("ga")
    core, y, x = me % 2, band // 2, band % 2
    across_x, across_y, diag = y * 2 + 1 - x, (1 - y) * 2 + x, 3 - band
    m = (1 - core) * y + core * x
    m_nbr = (1 - core) * across_y + core * across_x
    o_nbr = (1 - core) * across_x + core * across_y
    here = pl.multiple_of(m * half, LANES)
    there = pl.multiple_of((1 - m) * half, LANES)
    to_m, to_o = {"band": m_nbr}, {"band": o_nbr}

    def remote(src, dst, sems, device):
        return pltpu.make_async_remote_copy(
            src_ref=src, dst_ref=dst, send_sem=sems.at[0], recv_sem=sems.at[1],
            device_id=device, device_id_type=pl.DeviceIdType.MESH,
        )

    def span(k):
        return pl.ds(k * rows, rows)

    local_p = pltpu.make_async_copy(pj.at[:, pl.ds(here, half)], proj.at[0], s_loc.at[0])
    local_w = [
        pltpu.make_async_copy(wf.at[span(k), pl.ds(here, half)], wave.at[k, band], s_loc.at[1 + k])
        for k in range(chunks)
    ]
    send_p = remote(pj.at[:, pl.ds(there, half)], proj.at[1], s_p, to_m)
    send_wm = [
        remote(wf.at[span(k), pl.ds(there, half)], wave.at[k, band], s_wm.at[k], to_m)
        for k in range(chunks)
    ]
    send_wo = [
        remote(wf.at[span(k), pl.ds(here, half)], wave.at[k, band], s_wo.at[k], to_o)
        for k in range(chunks)
    ]
    send_wf = [
        remote(wave.at[k, m_nbr], wave.at[k, m_nbr], s_wf.at[k], to_o) for k in range(chunks)
    ]
    send_a = [remote(csend.at[k], crecv.at[k], s_a.at[k], to_m) for k in range(chunks)]
    send_f = [remote(mine.at[k], theirs.at[k], s_f.at[k], to_m) for k in range(chunks)]

    def peer(step):
        return (me + step + 1) % nga

    def send_c(k, step):
        return remote(
            sumb.at[k, peer(step)], parts.at[k, step], s_c.at[k, step], {"ga": peer(step)}
        )

    def send_d(k, step):
        return remote(mine.at[k, me], mine.at[k, me], s_d.at[k, step], {"ga": peer(step)})

    def send_n(k, t):
        return remote(nsend.at[k, t], nrecv.at[k, t], s_n.at[k, t], to_o)

    def send_o(k, t):
        place = out.at[span(k), pl.ds(pl.multiple_of(here + t * width, LANES), width)]
        return remote(nfull.at[k, t], place, s_o.at[k, t], to_m)

    def each_peer(body):
        def step(i, carry):
            body(i)
            return carry

        lax.fori_loop(0, nga - 1, step, 0)

    def each_tile(body, first=0, last=TILES):
        def step(i, carry):
            body(i)
            return carry

        lax.fori_loop(first, last, step, 0)

    def correlate(k, slot):
        acc[...] = jnp.zeros_like(acc)

        def tile(t):
            cols = pl.ds(pl.multiple_of(t * width, LANES), width)
            acc[...] += lax.dot_general(
                wave[k, :, :, cols].reshape(4 * rows, width),
                proj[slot, :, cols],
                (((1,), (1,)), ((), ())),
                preferred_element_type=jnp.float32,
            )

        each_tile(tile)

    def first(k):
        local_w[k].wait()
        send_wo[k].wait_recv()
        send_wf[k].wait_recv()
        if k == 0:
            correlate(k, 0)
            sumf[k] = acc[...].reshape(sumf.shape[1:])
            send_p.wait_recv()
        correlate(k, 1)
        csend[k] = acc[...].astype(jnp.bfloat16)
        send_a[k].start()
        if k > 0:
            correlate(k, 0)
            sumf[k] = acc[...].reshape(sumf.shape[1:])

    def reduce_start(k):
        send_a[k].wait_recv()
        total = sumf[k] + crecv[k].astype(jnp.float32).reshape(sumf.shape[1:])
        sumf[k] = total
        sumb[k] = total.astype(jnp.bfloat16)
        each_peer(lambda step: send_c(k, step).start())

    def mix_start(k):
        each_peer(lambda step: send_c(k, step).wait_recv())
        total = sumf[k, me]
        for step in range(nga - 1):
            total = total + parts[k, step].astype(jnp.float32)
        for t in range(tiles.shape[0]):
            cols = slice(t * LANES, (t + 1) * LANES)
            mine[k, me, :, cols] = jnp.dot(
                total[:, cols], tiles[t],
                preferred_element_type=jnp.float32, precision=lax.Precision.HIGHEST,
            ).astype(jnp.bfloat16)
        each_peer(lambda step: send_d(k, step).start())

    def share_start(k):
        each_peer(lambda step: send_d(k, step).wait_recv())
        send_f[k].start()

    def ordered(ref, k, blocks):
        picks = [ref[k, pl.ds(b * quarter, quarter)] for b in blocks]
        return jnp.concatenate(picks, axis=0).reshape(2 * rows, ref.shape[-1])

    def expand(k, t, blocks):
        cols = pl.ds(pl.multiple_of(t * width, LANES), width)
        value = jnp.dot(
            ordered(mine, k, blocks), proj[0, :, cols], preferred_element_type=jnp.float32
        )
        value += jnp.dot(
            ordered(theirs, k, blocks), proj[1, :, cols], preferred_element_type=jnp.float32
        )
        return value.reshape(2, rows, width)

    def second(k):
        send_f[k].wait_recv()

        def tile(t):
            nsend[k, t] = expand(k, t, (o_nbr, diag)).astype(jnp.bfloat16)
            send_n(k, t).start()

        each_tile(tile)

    def finish(k, begin, end):
        def tile(t):
            value = expand(k, t, (band, m_nbr))
            send_n(k, t).wait_recv()
            value += nrecv[k, t].astype(jnp.float32)
            nfull[k, t] = value[1].astype(jnp.bfloat16)
            send_o(k, t).start()
            cols = pl.ds(pl.multiple_of(here + t * width, LANES), width)
            out[span(k), cols] = value[0].astype(jnp.bfloat16)

        each_tile(tile, begin, end)

    local_p.start()
    for k in range(chunks):
        local_w[k].start()
    barrier = pltpu.get_barrier_semaphore()
    for device in (to_m, to_o):
        pl.semaphore_signal(
            barrier, inc=1, device_id=device, device_id_type=pl.DeviceIdType.MESH
        )
    each_peer(
        lambda step: pl.semaphore_signal(
            barrier, inc=1, device_id={"ga": peer(step)}, device_id_type=pl.DeviceIdType.MESH
        )
    )
    pl.semaphore_wait(barrier, nga + 1)

    send_wm[0].start()
    send_wo[0].start()
    send_p.start()
    for k in range(1, chunks):
        send_wm[k].start()
    send_wm[0].wait_recv()
    send_wf[0].start()
    for k in range(1, chunks):
        send_wo[k].start()
    local_p.wait()

    first(0)
    reduce_start(0)
    for k in range(1, chunks):
        send_wm[k].wait_recv()
        send_wf[k].start()
    mix_start(0)
    for k in range(1, chunks):
        share_start(k - 1)
        first(k)
        second(k - 1)
        reduce_start(k)
        mix_start(k)
        finish(k - 1, 0, TILES // 2)
        if k == chunks - 1:
            share_start(k)
        finish(k - 1, TILES // 2, TILES)
    if chunks == 1:
        share_start(0)
    second(chunks - 1)
    finish(chunks - 1, 0, TILES)

    send_p.wait_send()
    for k in range(chunks):
        for copy in (send_wm[k], send_wo[k], send_wf[k], send_a[k], send_f[k]):
            copy.wait_send()
        each_peer(lambda step: send_c(k, step).wait_send())
        each_peer(lambda step: send_d(k, step).wait_send())
        each_tile(lambda t: send_n(k, t).wait_send())
        each_tile(lambda t: send_o(k, t).wait())


def square(nga, wavefunctions, projectors, kinetic_diag, species_index, coupling):
    bands, waves = wavefunctions.shape
    count = projectors.shape[0]
    npa = coupling.shape[1]
    half, rows = waves // 2, bands // CHUNKS
    width, share = half // TILES, 4 * rows // nga
    tiles = mixing_tiles(
        species_index, coupling, lax.axis_index("band") * (count // npa), count // npa
    )
    bf16, f32 = jnp.bfloat16, jnp.float32
    dma = pltpu.SemaphoreType.DMA
    nonlocal_term = pl.pallas_call(
        functools.partial(kernel, nga),
        out_shape=jax.ShapeDtypeStruct((bands, waves), bf16),
        in_specs=[
            pl.BlockSpec(memory_space=pl.ANY),
            pl.BlockSpec(memory_space=pl.ANY),
            pl.BlockSpec(memory_space=pltpu.VMEM),
        ],
        out_specs=pl.BlockSpec(memory_space=pltpu.VMEM),
        scratch_shapes=[
            pltpu.VMEM((2, count, half), bf16),
            pltpu.VMEM((CHUNKS, 4, rows, half), bf16),
            pltpu.VMEM((4 * rows, count), f32),
            pltpu.VMEM((CHUNKS, 4 * rows, count), bf16),
            pltpu.VMEM((CHUNKS, 4 * rows, count), bf16),
            pltpu.VMEM((CHUNKS, nga, share, count), f32),
            pltpu.VMEM((CHUNKS, nga, share, count), bf16),
            pltpu.VMEM((CHUNKS, nga - 1, share, count), bf16),
            pltpu.VMEM((CHUNKS, nga, share, count), bf16),
            pltpu.VMEM((CHUNKS, nga, share, count), bf16),
            pltpu.VMEM((CHUNKS, TILES, 2, rows, width), bf16),
            pltpu.VMEM((CHUNKS, TILES, 2, rows, width), bf16),
            pltpu.VMEM((CHUNKS, TILES, rows, width), bf16),
            dma((1 + CHUNKS,)),
            dma((2,)),
            dma((CHUNKS, 2)),
            dma((CHUNKS, 2)),
            dma((CHUNKS, 2)),
            dma((CHUNKS, 2)),
            dma((CHUNKS, nga - 1, 2)),
            dma((CHUNKS, nga - 1, 2)),
            dma((CHUNKS, 2)),
            dma((CHUNKS, TILES, 2)),
            dma((CHUNKS, TILES, 2)),
        ],
        compiler_params=pltpu.CompilerParams(
            collective_id=0, has_side_effects=True, vmem_limit_bytes=60 * 2**20
        ),
    )(wavefunctions, projectors, tiles)
    return (
        kinetic_diag[None, :] * wavefunctions.astype(f32) + nonlocal_term.astype(f32)
    ).astype(bf16)


def solution(mesh):
    in_specs = (P("band", "ga"), P("band", "ga"), P("ga"), P(), P())
    out_specs = P("band", "ga")
    nga = mesh.shape["ga"]
    fits = mesh.shape["band"] == 4 and nga % 4 == 0
    body = functools.partial(square, nga) if fits else local
    return jax.shard_map(body, mesh=mesh, in_specs=in_specs, out_specs=out_specs, check_vma=False)
```

profile of v0, /device:TPU:28, one launch (start us, length us, event | category | flops | bytes accessed | tf_op | source)
XLA Modules:
  0.0 206.2 jit_solution(18082992797426148529)
XLA Ops:
  0.0 0.0 copy-start
  0.0 0.8 dynamic_slice.3
  0.8 0.1 broadcast_compare_fusion
  0.9 0.0 copy-done
  0.9 0.2 convolution_bitcast_fusion
  1.1 0.1 copy.8
  1.2 0.2 reshape.35
  1.4 0.7 bitcast_select_fusion.tiles
  2.1 0.0 copy-start.1
  2.1 0.0 copy-start.2
  2.1 199.6 %shard_map.55 = bf16[128,12288]{1,0:T(8,128)(2,1)} custom-call(bf16[128,12288]{1,0:T(8,128)(2,1)} %wf.1, bf16[512,12288]{1,0:T(8,128)(2,1)} %pj.1, f32[4,128,128]{2,1,0:T(8,128)} %bitcast_select_fusion.tiles), custom_call_target="tpu_custom_call" | custom-call | tf_op jit(solution)/shard_map/pallas_call | solution.py:309
  201.7 0.0 copy-done.1
  201.8 0.0 copy-done.2
  201.8 4.5 %add_convert_fusion = bf16[128,12288]{1,0:T(8,128)(2,1)} fusion(bf16[128,12288]{1,0:T(8,128)(2,1)} %shard_map.55, bf16[128,12288]{1,0:T(8,128)(2,1)S(1)} %copy-done.1, f32[12288]{0:T(1024)S(1)} %copy-done.2), kind=kLoop, calls=%fused_computation | loop fusion | flops 7864320 | bytes 9486336 | tf_op jit(solution)/shard_map/convert_element_type | solution.py:350
  (2 shorter events, 0.0 us)
Async XLA Ops:
  0.0 0.9 copy-start
  2.1 199.6 %copy-start.1 = (bf16[128,12288]{1,0:T(8,128)(2,1)S(1)}, bf16[128,12288]{1,0:T(8,128)(2,1)}, u32[]{:S(2)}) copy-start(bf16[128,12288]{1,0:T(8,128)(2,1)} %wf.1) | copy-start | bytes 9437188
  2.1 199.6 %copy-start.2 = (f32[12288]{0:T(1024)S(1)}, f32[12288]{0:T(1024)}, u32[]{:S(2)}) copy-start(f32[12288]{0:T(1024)} %param.7) | copy-start | bytes 147460
where the time goes:
time: 207 us; the launch traced here: 206 us
  Pallas kernels  200 us (97%)
  other arithmetic  5.29 us (3%)
    pallas_call x1, Pallas kernels, square(): pl.pallas_call(functools.partial(kernel, nga), out_shape=jax.ShapeDtypeSt...  200 us
    convert_element_type x1, other arithmetic, square(): return (kinetic_diag[None, :] * wavefunctions.astype(f32) + nonlocal_term...  4.48 us

commit v1 on v0

v1 whole, which is shorter than its diff:
```python
import functools

import jax
import jax.numpy as jnp
from jax import lax
from jax.experimental import pallas as pl
from jax.experimental.pallas import tpu as pltpu
from jax.sharding import PartitionSpec as P

CHUNKS = 4
TILES = 4
PIECES = 8
LANES = 128

NPA = 8


def apply_blocks(correlations, species_index, coupling, atom_start):
    rows = correlations.shape[0]
    count = correlations.shape[1] // NPA
    local_species = lax.dynamic_slice_in_dim(species_index, atom_start, count)
    onehot = (
        local_species[:, None] == jnp.arange(coupling.shape[0], dtype=jnp.int32)[None, :]
    ).astype(jnp.float32)
    blocks = jnp.einsum("as,sij->aij", onehot, coupling, precision=lax.Precision.HIGHEST)
    mixed = jnp.einsum(
        "baj,aij->bai",
        correlations.reshape(rows, count, NPA),
        blocks,
        precision=lax.Precision.HIGHEST,
    )
    return mixed.reshape(rows, count * NPA).astype(jnp.bfloat16)


def reduce_and_mix(partial_value, species_index, coupling, first_proj):
    total = lax.psum(partial_value.astype(jnp.bfloat16), "ga").astype(jnp.float32)
    return apply_blocks(total, species_index, coupling, first_proj // NPA)


def local(wavefunctions, projectors, kinetic_diag, species_index, coupling):
    proj_local = projectors.shape[0]
    band_index = lax.axis_index("band")
    partial_value = jnp.einsum(
        "bg,pg->bp",
        lax.all_gather(wavefunctions, "band", axis=0, tiled=True),
        projectors,
        preferred_element_type=jnp.float32,
    )
    mixed = reduce_and_mix(partial_value, species_index, coupling, band_index * proj_local)
    nonlocal_term = lax.psum_scatter(
        jnp.dot(mixed, projectors, preferred_element_type=jnp.float32).astype(jnp.bfloat16),
        "band",
        scatter_dimension=0,
        tiled=True,
    ).astype(jnp.float32)
    return (kinetic_diag[None, :] * wavefunctions.astype(jnp.float32) + nonlocal_term).astype(
        jnp.bfloat16
    )


def schedule(chunks):
    period = 50.0 / chunks
    events = []
    for k in range(chunks):
        ready = 0.0 if k == 0 else k * period + 4.0
        if k > 0:
            events.append((ready - 10.0, "forward", k))
        events.append((ready, "correlate", k))
        events.append((ready + 10.0, "reduce", k))
        events.append((ready + 12.5, "join", k))
        events.append((ready + 13.7, "mix", k))
        if k == 0:
            events.append((ready + 13.8, "feed", k))
        events.append((ready + 16.0, "share", k))
        events.append((ready + 26.0, "expand", k))
        for t in range(TILES):
            events.append((ready + 38.0 + 2.5 * t, "finish", (k, t)))
    return [event[1:] for event in sorted(events, key=lambda event: event[0])]


def kernel(
    nga, wf, pj, kin_hbm, species_hbm, coupling_hbm, out,
    proj, wave, acc, csend, keep, parts, msend, mrecv, dsend, drecv, mixed,
    nsend, nrecv, own, nfull, kin, species, coupling, tiles,
    s_loc, s_p, s_wm, s_wo, s_wf, s_z, s_m, s_d, s_b, s_e, s_g, s_n, s_o,
):
    chunks, _, rows, half = wave.shape
    _, zn, share, both = csend.shape
    count = both // 2
    width = nsend.shape[-1]
    piece = half // PIECES
    quarter = zn // 4
    band, me = lax.axis_index("band"), lax.axis_index("ga")
    core, z, y, x = me % 2, me // 2, band // 2, band % 2
    across_x, across_y, diag = y * 2 + 1 - x, (1 - y) * 2 + x, 3 - band
    m = (1 - core) * y + core * x
    m_nbr = (1 - core) * across_y + core * across_x
    o_nbr = (1 - core) * across_x + core * across_y
    here = pl.multiple_of(m * half, LANES)
    there = pl.multiple_of((1 - m) * half, LANES)
    to_m, to_o, to_twin = {"band": m_nbr}, {"band": o_nbr}, {"ga": z * 2 + 1 - core}

    def remote(src, dst, sems, device):
        return pltpu.make_async_remote_copy(
            src_ref=src, dst_ref=dst, send_sem=sems.at[0], recv_sem=sems.at[1],
            device_id=device, device_id_type=pl.DeviceIdType.MESH,
        )

    def span(k):
        return pl.ds(k * rows, rows)

    def peer(step):
        return (z + 1 + step) % zn

    def to_peer(step):
        return {"ga": peer(step) * 2 + core}

    local_p = pltpu.make_async_copy(pj.at[:, pl.ds(here, half)], proj.at[0], s_loc.at[0])
    local_k = pltpu.make_async_copy(kin_hbm.at[:, pl.ds(here, half)], kin, s_loc.at[1])
    local_s = pltpu.make_async_copy(species_hbm, species, s_loc.at[2])
    local_c = pltpu.make_async_copy(coupling_hbm, coupling, s_loc.at[3])
    local_w = [
        pltpu.make_async_copy(wf.at[span(k), pl.ds(here, half)], wave.at[k, band], s_loc.at[4 + k])
        for k in range(chunks)
    ]
    send_p = [
        remote(
            pj.at[:, pl.ds(pl.multiple_of(there + i * piece, LANES), piece)],
            proj.at[1, :, pl.ds(i * piece, piece)], s_p.at[i], to_m,
        )
        for i in range(PIECES)
    ]
    send_wm = [
        remote(wf.at[span(k), pl.ds(there, half)], wave.at[k, band], s_wm.at[k], to_m)
        for k in range(chunks)
    ]
    send_wo = [
        remote(wf.at[span(k), pl.ds(here, half)], wave.at[k, band], s_wo.at[k], to_o)
        for k in range(chunks)
    ]
    send_wf = [
        remote(wave.at[k, m_nbr], wave.at[k, m_nbr], s_wf.at[k], to_o) for k in range(chunks)
    ]
    send_m = [remote(msend.at[k], mrecv.at[k], s_m.at[k], to_m) for k in range(chunks)]
    send_d = [remote(dsend.at[k], drecv.at[k], s_d.at[k], to_twin) for k in range(chunks)]
    send_b = [
        remote(mixed.at[k, z, :, :count], mixed.at[k, z, :, count:], s_b.at[k], to_m)
        for k in range(chunks)
    ]

    def send_z(k, step):
        return remote(
            csend.at[k, peer(step)], parts.at[k, step], s_z.at[k, step], to_peer(step)
        )

    def send_e(k, step):
        place = mixed.at[k, z, :, :count]
        return remote(place, place, s_e.at[k, step], to_peer(step))

    def send_g(k, step):
        place = mixed.at[k, z, :, count:]
        return remote(place, place, s_g.at[k, step], to_peer(step))

    def send_n(k, t):
        return remote(nsend.at[k, t], nrecv.at[k, t], s_n.at[k, t], to_o)

    def send_o(k, t):
        place = out.at[span(k), pl.ds(pl.multiple_of(here + t * width, LANES), width)]
        return remote(nfull.at[k, t], place, s_o.at[k, t], to_m)

    def each_peer(body):
        def step(i, carry):
            body(i)
            return carry

        lax.fori_loop(0, zn - 1, step, 0)

    def each_tile(body):
        def step(i, carry):
            body(i)
            return carry

        lax.fori_loop(0, TILES, step, 0)

    def columns(t):
        return pl.ds(pl.multiple_of(t * width, LANES), width)

    def add_product(k, slot, cols):
        product = lax.dot_general(
            wave[k, :, :, cols].reshape(4 * rows, -1),
            proj[slot, :, cols],
            (((1,), (1,)), ((), ())),
            preferred_element_type=jnp.float32,
        )
        acc[:, :, slot * count : (slot + 1) * count] += product.reshape(zn, share, count)

    def build_tiles():
        kinds, npa = coupling.shape[0], coupling.shape[1]
        atoms = species.shape[1]
        local_s.wait()
        local_c.wait()
        first = band * (count // npa)
        atom = lax.broadcasted_iota(jnp.int32, (atoms, count), 0)
        column = lax.broadcasted_iota(jnp.int32, (atoms, count), 1)
        spread = (atom == first + column // npa).astype(jnp.float32)
        kind = lax.broadcasted_iota(jnp.int32, (8, atoms), 0)
        onehot = (kind == species[...]).astype(jnp.float32)
        chosen = jnp.dot(
            onehot, spread, preferred_element_type=jnp.float32, precision=lax.Precision.HIGHEST
        )
        row = lax.broadcasted_iota(jnp.int32, (LANES, npa), 0)
        index = lax.broadcasted_iota(jnp.int32, (LANES, npa), 1)
        repeat = (row % npa == index).astype(jnp.float32)
        blocks = []
        for s in range(kinds):
            tall = lax.dot_general(
                repeat, coupling[s], (((1,), (1,)), ((), ())),
                preferred_element_type=jnp.float32, precision=lax.Precision.HIGHEST,
            )
            blocks.append(
                lax.dot_general(
                    tall, repeat, (((1,), (1,)), ((), ())),
                    preferred_element_type=jnp.float32, precision=lax.Precision.HIGHEST,
                )
            )
        atom_row = lax.broadcasted_iota(jnp.int32, (LANES, LANES), 0) // npa
        atom_col = lax.broadcasted_iota(jnp.int32, (LANES, LANES), 1) // npa
        same = atom_row == atom_col
        for t in range(tiles.shape[0]):
            value = jnp.zeros((LANES, LANES), jnp.float32)
            for s in range(kinds):
                here_kind = chosen[s : s + 1, t * LANES : (t + 1) * LANES]
                value = jnp.where(here_kind > 0.5, blocks[s], value)
            tiles[t] = jnp.where(same, value, 0.0)

    def forward(k):
        send_wm[k].wait_recv()
        send_wf[k].start()

    def feed(k):
        for later in range(2, chunks):
            send_wm[later].start()

    def correlate(k):
        if k > 0:
            local_w[k].wait()
            send_wo[k].wait_recv()
            send_wf[k].wait_recv()
            acc[...] = jnp.zeros_like(acc)

            def tile(t):
                add_product(k, 0, columns(t))
                add_product(k, 1, columns(t))

            each_tile(tile)
        csend[k] = acc[...].astype(jnp.bfloat16)
        each_peer(lambda step: send_z(k, step).start())
        keep[k] = acc[z]

    def reduce(k):
        each_peer(lambda step: send_z(k, step).wait_recv())
        total = keep[k]
        for step in range(zn - 1):
            total = total + parts[k, step].astype(jnp.float32)
        msend[k] = total[:, count:].astype(jnp.bfloat16)
        send_m[k].start()
        dsend[k] = total[:, :count]

    def join(k):
        send_m[k].wait_recv()
        dsend[k] = dsend[k] + mrecv[k].astype(jnp.float32)
        send_d[k].start()

    def mix(k):
        send_d[k].wait_recv()
        total = dsend[k] + drecv[k]
        for t in range(tiles.shape[0]):
            cols = slice(t * LANES, (t + 1) * LANES)
            mixed[k, z, :, cols] = jnp.dot(
                total[:, cols], tiles[t],
                preferred_element_type=jnp.float32, precision=lax.Precision.HIGHEST,
            ).astype(jnp.bfloat16)
        send_b[k].start()
        each_peer(lambda step: send_e(k, step).start())

    def share_out(k):
        send_b[k].wait_recv()
        each_peer(lambda step: send_g(k, step).start())

    def expand(k):
        each_peer(lambda step: send_e(k, step).wait_recv())
        each_peer(lambda step: send_g(k, step).wait_recv())

        def tile(t):
            cols = columns(t)
            picks = [
                mixed[k, pl.ds(b * quarter, quarter)].reshape(rows, both)
                for b in (o_nbr, diag, band, m_nbr)
            ]
            value = jnp.dot(
                jnp.concatenate(picks, axis=0), proj[:, :, cols].reshape(both, width),
                preferred_element_type=jnp.float32,
            ).reshape(4, rows, width)
            nsend[k, t] = value[:2].astype(jnp.bfloat16)
            send_n(k, t).start()
            own[k, t] = value[2:]

        each_tile(tile)

    def finish(k, t):
        send_n(k, t).wait_recv()
        cols = columns(t)
        scale = kin[:, cols]
        value = own[k, t] + nrecv[k, t].astype(jnp.float32)
        theirs = scale * wave[k, m_nbr, :, cols].astype(jnp.float32) + value[1]
        nfull[k, t] = theirs.astype(jnp.bfloat16)
        send_o(k, t).start()
        mine = scale * wave[k, band, :, cols].astype(jnp.float32) + value[0]
        place = pl.ds(pl.multiple_of(here + t * width, LANES), width)
        out[span(k), place] = mine.astype(jnp.bfloat16)

    barrier = pltpu.get_barrier_semaphore()
    for device in (to_m, to_o, to_twin):
        pl.semaphore_signal(
            barrier, inc=1, device_id=device, device_id_type=pl.DeviceIdType.MESH
        )
    each_peer(
        lambda step: pl.semaphore_signal(
            barrier, inc=1, device_id=to_peer(step), device_id_type=pl.DeviceIdType.MESH
        )
    )
    local_p.start()
    for copy in local_w:
        copy.start()
    local_s.start()
    local_c.start()
    local_k.start()
    pl.semaphore_wait(barrier, zn + 2)

    send_wm[0].start()
    send_wo[0].start()
    for copy in send_p:
        copy.start()
    send_wm[1].start()
    build_tiles()
    forward(0)
    local_k.wait()
    local_p.wait()
    local_w[0].wait()
    send_wo[0].wait_recv()
    send_wf[0].wait_recv()
    acc[...] = jnp.zeros_like(acc)
    each_tile(lambda t: add_product(0, 0, columns(t)))
    for i in range(PIECES):
        send_p[i].wait_recv()
        if i == PIECES - 2:
            for k in range(1, chunks):
                send_wo[k].start()
        add_product(0, 1, slice(i * piece, (i + 1) * piece))

    stages = {
        "forward": forward, "correlate": correlate, "reduce": reduce, "join": join,
        "mix": mix, "feed": feed, "share": share_out, "expand": expand,
    }
    for stage, at in schedule(chunks):
        if stage == "finish":
            finish(*at)
        else:
            stages[stage](at)

    for copy in send_p:
        copy.wait_send()
    for k in range(chunks):
        for copy in (send_wm[k], send_wo[k], send_wf[k], send_m[k], send_d[k], send_b[k]):
            copy.wait_send()
        for send in (send_z, send_e, send_g):
            each_peer(lambda step: send(k, step).wait_send())
        each_tile(lambda t: send_n(k, t).wait_send())
        each_tile(lambda t: send_o(k, t).wait())


def square(nga, wavefunctions, projectors, kinetic_diag, species_index, coupling):
    bands, waves = wavefunctions.shape
    count = projectors.shape[0]
    atoms = species_index.shape[0]
    half, rows = waves // 2, bands // CHUNKS
    zn = nga // 2
    width, share = half // TILES, 4 * rows // zn
    bf16, f32 = jnp.bfloat16, jnp.float32
    dma = pltpu.SemaphoreType.DMA
    anywhere = pl.BlockSpec(memory_space=pl.ANY)
    return pl.pallas_call(
        functools.partial(kernel, nga),
        out_shape=jax.ShapeDtypeStruct((bands, waves), bf16),
        in_specs=[anywhere] * 5,
        out_specs=pl.BlockSpec(memory_space=pltpu.VMEM),
        scratch_shapes=[
            pltpu.VMEM((2, count, half), bf16),
            pltpu.VMEM((CHUNKS, 4, rows, half), bf16),
            pltpu.VMEM((zn, share, 2 * count), f32),
            pltpu.VMEM((CHUNKS, zn, share, 2 * count), bf16),
            pltpu.VMEM((CHUNKS, share, 2 * count), f32),
            pltpu.VMEM((CHUNKS, zn - 1, share, 2 * count), bf16),
            pltpu.VMEM((CHUNKS, share, count), bf16),
            pltpu.VMEM((CHUNKS, share, count), bf16),
            pltpu.VMEM((CHUNKS, share, count), f32),
            pltpu.VMEM((CHUNKS, share, count), f32),
            pltpu.VMEM((CHUNKS, zn, share, 2 * count), bf16),
            pltpu.VMEM((CHUNKS, TILES, 2, rows, width), bf16),
            pltpu.VMEM((CHUNKS, TILES, 2, rows, width), bf16),
            pltpu.VMEM((CHUNKS, TILES, 2, rows, width), f32),
            pltpu.VMEM((CHUNKS, TILES, rows, width), bf16),
            pltpu.VMEM((1, half), f32),
            pltpu.VMEM((1, atoms), jnp.int32),
            pltpu.VMEM(coupling.shape, f32),
            pltpu.VMEM((count // LANES, LANES, LANES), f32),
            dma((4 + CHUNKS,)),
            dma((PIECES, 2)),
            dma((CHUNKS, 2)),
            dma((CHUNKS, 2)),
            dma((CHUNKS, 2)),
            dma((CHUNKS, zn - 1, 2)),
            dma((CHUNKS, 2)),
            dma((CHUNKS, 2)),
            dma((CHUNKS, 2)),
            dma((CHUNKS, zn - 1, 2)),
            dma((CHUNKS, zn - 1, 2)),
            dma((CHUNKS, TILES, 2)),
            dma((CHUNKS, TILES, 2)),
        ],
        compiler_params=pltpu.CompilerParams(
            collective_id=0, has_side_effects=True, vmem_limit_bytes=50 * 2**20
        ),
    )(
        wavefunctions, projectors, kinetic_diag.reshape(1, waves),
        species_index.reshape(1, atoms), coupling,
    )


def solution(mesh):
    in_specs = (P("band", "ga"), P("band", "ga"), P("ga"), P(), P())
    out_specs = P("band", "ga")
    nga = mesh.shape["ga"]
    fits = mesh.shape["band"] == 4 and nga % 8 == 0
    body = functools.partial(square, nga) if fits else local
    return jax.shard_map(body, mesh=mesh, in_specs=in_specs, out_specs=out_specs, check_vma=False)
```

time: 207 us -> 198 us (0.957)
  Pallas kernels: 200 us -> 192 us
  other arithmetic: 5.29 us -> 0 us
  local copies, waits for them, and re-layouts: 1.07 us -> 3.86 us
    pallas_call x1, Pallas kernels: 200 us -> 192 us  [square(): pl.pallas_call(functools.partial(kernel, nga), out_shape=jax.ShapeDtypeSt...]
    convert_element_type x1 -> x0, other arithmetic: 4.48 us -> none  [square(): return (kinetic_diag[None, :] * wavefunctions.astype(f32) + nonlocal_term...]
    unnamed x6 -> x7, local copies, waits for them, and re-layouts: 0.01 us -> 3.86 us
where the time goes in v1:
time: 198 us; the launch traced here: 196 us
  Pallas kernels  192 us (97%)
  local copies, waits for them, and re-layouts  3.86 us (2%)
    pallas_call x1, Pallas kernels, square(): pl.pallas_call(functools.partial(kernel, nga), out_shape=jax.ShapeDtypeSt...  192 us

profile of v1, /device:TPU:28, one launch (start us, length us, event | category | flops | bytes accessed | tf_op | source)
XLA Modules:
  0.0 196.0 jit_solution(13249322999738670347)
XLA Ops:
  0.0 0.0 copy-start
  0.0 0.8 copy-done
  0.8 0.0 copy-start.1
  0.8 0.7 copy-done.1
  1.5 0.0 copy-start.2
  1.5 0.7 copy-done.2
  2.2 192.2 %shard_map.55 = bf16[128,12288]{1,0:T(8,128)(2,1)S(1)} custom-call(bf16[128,12288]{1,0:T(8,128)(2,1)} %wf.1, bf16[512,12288]{1,0:T(8,128)(2,1)} %pj.1, f32[1,12288]{1,0:T(1,128)S(1)} %bitcast.2, s32[1,256]{1,0:T(1,128)S(1)} %bitcast.3, f32[4,8,8]{2,1,0:T(8,128)S(1)} %copy-done.1), custom_call_target="tpu_custom_call" | custom-call | tf_op jit(solution)/shard_map/pallas_call | solution.py:392
  194.4 1.7 copy.7
Async XLA Ops:
  0.0 0.8 copy-start
  0.8 0.7 copy-start.1
  1.5 0.7 copy-start.2

commit v2 on v1

--- a/solution.py
+++ b/solution.py
@@ -58,31 +58,38 @@
     )
 
 
-def schedule(chunks):
-    period = 50.0 / chunks
-    events = []
-    for k in range(chunks):
-        ready = 0.0 if k == 0 else k * period + 4.0
-        if k > 0:
-            events.append((ready - 10.0, "forward", k))
-        events.append((ready, "correlate", k))
-        events.append((ready + 10.0, "reduce", k))
-        events.append((ready + 12.5, "join", k))
-        events.append((ready + 13.7, "mix", k))
-        if k == 0:
-            events.append((ready + 13.8, "feed", k))
-        events.append((ready + 16.0, "share", k))
-        events.append((ready + 26.0, "expand", k))
-        for t in range(TILES):
-            events.append((ready + 38.0 + 2.5 * t, "finish", (k, t)))
-    return [event[1:] for event in sorted(events, key=lambda event: event[0])]
+EARLY = 2
+
+
+def schedule():
+    times = {
+        "correlate": (0.3, 0.5, 16.5, 24.6),
+        "forward": (None, None, 4.0, 9.5),
+        "reduce": (7.5, 12.0, 29.3, 37.4),
+        "join": (9.7, 15.0, 32.2, 40.0),
+        "mix": (11.3, 21.2, 33.4, 41.2),
+        "share": (14.4, 24.0, 36.0, 44.0),
+        "expand": (21.5, 29.6, 42.0, 50.0),
+        "settle": (57.0, None, None, None),
+    }
+    events = [
+        (at, stage, k, 0)
+        for stage, row in times.items()
+        for k, at in enumerate(row)
+        if at is not None
+    ]
+    for k, (first, step) in enumerate(((29.5, 0.02), (36.5, 1.2), (50.5, 1.2), (62.0, 1.0))):
+        events += [(first + step * t, "far", k, t) for t in range(TILES)]
+    for k, first in enumerate((44.2, 52.6, 58.0, 70.0)):
+        events += [(first + 0.05 * t, "near", k, t) for t in range(TILES)]
+    return [event[1:] for event in sorted(events)]
 
 
 def kernel(
     nga, wf, pj, kin_hbm, species_hbm, coupling_hbm, out,
     proj, wave, acc, csend, keep, parts, msend, mrecv, dsend, drecv, mixed,
-    nsend, nrecv, own, nfull, kin, species, coupling, tiles,
-    s_loc, s_p, s_wm, s_wo, s_wf, s_z, s_m, s_d, s_b, s_e, s_g, s_n, s_o,
+    nsend, nrecv, own, nfull, ready, kin, species, coupling, tiles,
+    s_loc, s_p, s_wm, s_wo, s_wf, s_z, s_m, s_d, s_b, s_e, s_g, s_n, s_o, s_w,
 ):
     chunks, _, rows, half = wave.shape
     _, zn, share, both = csend.shape
@@ -161,12 +168,17 @@
         place = mixed.at[k, z, :, count:]
         return remote(place, place, s_g.at[k, step], to_peer(step))
 
-    def send_n(k, t):
-        return remote(nsend.at[k, t], nrecv.at[k, t], s_n.at[k, t], to_o)
+    def send_n(k, t, side):
+        return remote(nsend.at[k, t, side], nrecv.at[k, t, side], s_n.at[k, t, side], to_o)
+
+    def place(k, t):
+        return out.at[span(k), pl.ds(pl.multiple_of(here + t * width, LANES), width)]
 
     def send_o(k, t):
-        place = out.at[span(k), pl.ds(pl.multiple_of(here + t * width, LANES), width)]
-        return remote(nfull.at[k, t], place, s_o.at[k, t], to_m)
+        return remote(nfull.at[k, t], place(k, t), s_o.at[k, t], to_m)
+
+    def write(k, t):
+        return pltpu.make_async_copy(ready.at[k, t], place(k, t), s_w.at[k, t])
 
     def each_peer(body):
         def step(i, carry):
@@ -185,14 +197,15 @@
     def columns(t):
         return pl.ds(pl.multiple_of(t * width, LANES), width)
 
-    def add_product(k, slot, cols):
+    def add_product(chunk, slot, cols):
         product = lax.dot_general(
-            wave[k, :, :, cols].reshape(4 * rows, -1),
+            wave[chunk, :, :, cols].reshape(-1, proj[slot, :, cols].shape[-1]),
             proj[slot, :, cols],
             (((1,), (1,)), ((), ())),
             preferred_element_type=jnp.float32,
         )
-        acc[:, :, slot * count : (slot + 1) * count] += product.reshape(zn, share, count)
+        product = product.reshape(-1, zn, share, count)
+        acc[: product.shape[0], :, :, slot * count : (slot + 1) * count] += product
 
     def build_tiles():
         kinds, npa = coupling.shape[0], coupling.shape[1]
@@ -235,27 +248,30 @@
 
     def forward(k):
         send_wm[k].wait_recv()
+        if k == EARLY:
+            send_wo[k].start()
         send_wf[k].start()
-
-    def feed(k):
-        for later in range(2, chunks):
-            send_wm[later].start()
+        if k == EARLY:
+            for later in range(EARLY + 1, chunks):
+                send_wo[later].start()
 
     def correlate(k):
-        if k > 0:
+        place = k
+        if k >= EARLY:
+            place = 0
             local_w[k].wait()
             send_wo[k].wait_recv()
             send_wf[k].wait_recv()
-            acc[...] = jnp.zeros_like(acc)
+            acc[0] = jnp.zeros_like(acc[0])
 
             def tile(t):
-                add_product(k, 0, columns(t))
-                add_product(k, 1, columns(t))
+                add_product(slice(k, k + 1), 0, columns(t))
+                add_product(slice(k, k + 1), 1, columns(t))
 
             each_tile(tile)
-        csend[k] = acc[...].astype(jnp.bfloat16)
+        csend[k] = acc[place].astype(jnp.bfloat16)
         each_peer(lambda step: send_z(k, step).start())
-        keep[k] = acc[z]
+        keep[k] = acc[place, z]
 
     def reduce(k):
         each_peer(lambda step: send_z(k, step).wait_recv())
@@ -302,22 +318,26 @@
                 preferred_element_type=jnp.float32,
             ).reshape(4, rows, width)
             nsend[k, t] = value[:2].astype(jnp.bfloat16)
-            send_n(k, t).start()
+            send_n(k, t, 1).start()
             own[k, t] = value[2:]
 
         each_tile(tile)
-
-    def finish(k, t):
-        send_n(k, t).wait_recv()
+        each_tile(lambda t: send_n(k, t, 0).start())
+
+    def complete(k, t, side, owner):
+        send_n(k, t, side).wait_recv()
         cols = columns(t)
-        scale = kin[:, cols]
-        value = own[k, t] + nrecv[k, t].astype(jnp.float32)
-        theirs = scale * wave[k, m_nbr, :, cols].astype(jnp.float32) + value[1]
-        nfull[k, t] = theirs.astype(jnp.bfloat16)
+        kinetic = kin[:, cols] * wave[k, owner, :, cols].astype(jnp.float32)
+        total = own[k, t, side] + nrecv[k, t, side].astype(jnp.float32)
+        return (kinetic + total).astype(jnp.bfloat16)
+
+    def far(k, t):
+        nfull[k, t] = complete(k, t, 1, m_nbr)
         send_o(k, t).start()
-        mine = scale * wave[k, band, :, cols].astype(jnp.float32) + value[0]
-        place = pl.ds(pl.multiple_of(here + t * width, LANES), width)
-        out[span(k), place] = mine.astype(jnp.bfloat16)
+
+    def near(k, t):
+        ready[k, t] = complete(k, t, 0, band)
+        write(k, t).start()
 
     barrier = pltpu.get_barrier_semaphore()
     for device in (to_m, to_o, to_twin):
@@ -337,46 +357,64 @@
     local_k.start()
     pl.semaphore_wait(barrier, zn + 2)
 
-    send_wm[0].start()
-    send_wo[0].start()
+    for k in range(EARLY):
+        send_wm[k].start()
+        send_wo[k].start()
     for copy in send_p:
         copy.start()
-    send_wm[1].start()
-    build_tiles()
-    forward(0)
-    local_k.wait()
-    local_p.wait()
-    local_w[0].wait()
-    send_wo[0].wait_recv()
-    send_wf[0].wait_recv()
-    acc[...] = jnp.zeros_like(acc)
-    each_tile(lambda t: add_product(0, 0, columns(t)))
+    for k in range(EARLY, chunks):
+        send_wm[k].start()
+    with jax.named_scope("build"):
+        build_tiles()
+    with jax.named_scope("first"):
+        for k in range(EARLY):
+            forward(k)
+        local_k.wait()
+        local_p.wait()
+        for k in range(EARLY):
+            local_w[k].wait()
+            send_wo[k].wait_recv()
+            send_wf[k].wait_recv()
+        acc[...] = jnp.zeros_like(acc)
+        each_tile(lambda t: add_product(slice(0, EARLY), 0, columns(t)))
     for i in range(PIECES):
-        send_p[i].wait_recv()
-        if i == PIECES - 2:
-            for k in range(1, chunks):
-                send_wo[k].start()
-        add_product(0, 1, slice(i * piece, (i + 1) * piece))
+        with jax.named_scope(f"piece#i={i}"):
+            send_p[i].wait_recv()
+            add_product(slice(0, EARLY), 1, slice(i * piece, (i + 1) * piece))
+
+    def settle(k):
+        for copy in send_p:
+            copy.wait_send()
+        for i in range(chunks):
+            for copy in (send_wm[i], send_wo[i], send_wf[i], send_m[i], send_d[i], send_b[i]):
+                copy.wait_send()
+            for send in (send_z, send_e, send_g):
+                each_peer(lambda step: send(i, step).wait_send())
+        for i in range(chunks - 1):
+            each_tile(lambda t: send_n(i, t, 0).wait_send())
+            each_tile(lambda t: send_n(i, t, 1).wait_send())
 
     stages = {
-        "forward": forward, "correlate": correlate, "reduce": reduce, "join": join,
-        "mix": mix, "feed": feed, "share": share_out, "expand": expand,
+        "forward": forward, "correlate": correlate, "reduce": reduce, "join": join, "mix": mix,
+        "share": share_out, "expand": expand, "settle": settle,
     }
-    for stage, at in schedule(chunks):
-        if stage == "finish":
-            finish(*at)
-        else:
-            stages[stage](at)
-
-    for copy in send_p:
-        copy.wait_send()
-    for k in range(chunks):
-        for copy in (send_wm[k], send_wo[k], send_wf[k], send_m[k], send_d[k], send_b[k]):
-            copy.wait_send()
-        for send in (send_z, send_e, send_g):
-            each_peer(lambda step: send(k, step).wait_send())
-        each_tile(lambda t: send_n(k, t).wait_send())
-        each_tile(lambda t: send_o(k, t).wait())
+    for stage, k, t in schedule():
+        with jax.named_scope(f"{stage}#k={k}#t={t}"):
+            if stage == "far":
+                far(k, t)
+            elif stage == "near":
+                near(k, t)
+            else:
+                stages[stage](k)
+    with jax.named_scope("others"):
+        for k in range(chunks - 1):
+            each_tile(lambda t: send_o(k, t).wait())
+        for k in range(chunks):
+            each_tile(lambda t: write(k, t).wait())
+    for side in range(2):
+        each_tile(lambda t: send_n(chunks - 1, t, side).wait_send())
+    with jax.named_scope("last"):
+        each_tile(lambda t: send_o(chunks - 1, t).wait())
 
 
 def square(nga, wavefunctions, projectors, kinetic_diag, species_index, coupling):
@@ -393,11 +431,11 @@
         functools.partial(kernel, nga),
         out_shape=jax.ShapeDtypeStruct((bands, waves), bf16),
         in_specs=[anywhere] * 5,
-        out_specs=pl.BlockSpec(memory_space=pltpu.VMEM),
+        out_specs=anywhere,
         scratch_shapes=[
             pltpu.VMEM((2, count, half), bf16),
             pltpu.VMEM((CHUNKS, 4, rows, half), bf16),
-            pltpu.VMEM((zn, share, 2 * count), f32),
+            pltpu.VMEM((EARLY, zn, share, 2 * count), f32),
             pltpu.VMEM((CHUNKS, zn, share, 2 * count), bf16),
             pltpu.VMEM((CHUNKS, share, 2 * count), f32),
             pltpu.VMEM((CHUNKS, zn - 1, share, 2 * count), bf16),
@@ -410,6 +448,7 @@
             pltpu.VMEM((CHUNKS, TILES, 2, rows, width), bf16),
             pltpu.VMEM((CHUNKS, TILES, 2, rows, width), f32),
             pltpu.VMEM((CHUNKS, TILES, rows, width), bf16),
+            pltpu.VMEM((CHUNKS, TILES, rows, width), bf16),
             pltpu.VMEM((1, half), f32),
             pltpu.VMEM((1, atoms), jnp.int32),
             pltpu.VMEM(coupling.shape, f32),
@@ -425,8 +464,9 @@
             dma((CHUNKS, 2)),
             dma((CHUNKS, zn - 1, 2)),
             dma((CHUNKS, zn - 1, 2)),
+            dma((CHUNKS, TILES, 2, 2)),
             dma((CHUNKS, TILES, 2)),
-            dma((CHUNKS, TILES, 2)),
+            dma((CHUNKS, TILES)),
         ],
         compiler_params=pltpu.CompilerParams(
             collective_id=0, has_side_effects=True, vmem_limit_bytes=50 * 2**20

time: 198 us -> 186 us (0.939)
  Pallas kernels: 192 us -> 181 us
    pallas_call x1, Pallas kernels: 192 us -> 181 us  [square(): pl.pallas_call(functools.partial(kernel, nga), out_shape=jax.ShapeDtypeSt...]
where the time goes in v2:
time: 186 us; the launch traced here: 185 us
  Pallas kernels  181 us (97%)
  local copies, waits for them, and re-layouts  3.86 us (2%)
    pallas_call x1, Pallas kernels, square(): pl.pallas_call(functools.partial(kernel, nga), out_shape=jax.ShapeDtypeSt...  181 us
    unnamed x7, local copies, waits for them, and re-layouts  3.86 us

profile of v2, /device:TPU:28, one launch (start us, length us, event | category | flops | bytes accessed | tf_op | source)
XLA Modules:
  0.0 184.7 jit_solution(14454231025636835953)
XLA Ops:
  0.0 0.0 copy-start
  0.0 0.8 copy-done
  0.8 0.0 copy-start.1
  0.8 0.7 copy-done.1
  1.5 0.0 copy-start.2
  1.5 0.7 copy-done.2
  2.2 180.8 %shard_map.55 = bf16[128,12288]{1,0:T(8,128)(2,1)S(1)} custom-call(bf16[128,12288]{1,0:T(8,128)(2,1)} %wf.1, bf16[512,12288]{1,0:T(8,128)(2,1)} %pj.1, f32[1,12288]{1,0:T(1,128)S(1)} %bitcast.2, s32[1,256]{1,0:T(1,128)S(1)} %bitcast.3, f32[4,8,8]{2,1,0:T(8,128)S(1)} %copy-done.1), custom_call_target="tpu_custom_call" | custom-call | tf_op jit(solution)/shard_map/pallas_call | solution.py:430
  183.0 1.7 copy.7
Async XLA Ops:
  0.0 0.8 copy-start
  0.8 0.7 copy-start.1
  1.5 0.7 copy-start.2

commit v3 on v2

--- a/solution.py
+++ b/solution.py
@@ -89,7 +89,7 @@
     nga, wf, pj, kin_hbm, species_hbm, coupling_hbm, out,
     proj, wave, acc, csend, keep, parts, msend, mrecv, dsend, drecv, mixed,
     nsend, nrecv, own, nfull, ready, kin, species, coupling, tiles,
-    s_loc, s_p, s_wm, s_wo, s_wf, s_z, s_m, s_d, s_b, s_e, s_g, s_n, s_o, s_w,
+    s_send, s_loc, s_p, s_wm, s_wo, s_m, s_d, s_b, s_z, s_e, s_far, s_near, s_out,
 ):
     chunks, _, rows, half = wave.shape
     _, zn, share, both = csend.shape
@@ -107,9 +107,9 @@
     there = pl.multiple_of((1 - m) * half, LANES)
     to_m, to_o, to_twin = {"band": m_nbr}, {"band": o_nbr}, {"ga": z * 2 + 1 - core}
 
-    def remote(src, dst, sems, device):
+    def remote(src, dst, sent, received, device):
         return pltpu.make_async_remote_copy(
-            src_ref=src, dst_ref=dst, send_sem=sems.at[0], recv_sem=sems.at[1],
+            src_ref=src, dst_ref=dst, send_sem=s_send.at[sent], recv_sem=received,
             device_id=device, device_id_type=pl.DeviceIdType.MESH,
         )
 
@@ -127,58 +127,69 @@
     local_s = pltpu.make_async_copy(species_hbm, species, s_loc.at[2])
     local_c = pltpu.make_async_copy(coupling_hbm, coupling, s_loc.at[3])
     local_w = [
-        pltpu.make_async_copy(wf.at[span(k), pl.ds(here, half)], wave.at[k, band], s_loc.at[4 + k])
+        pltpu.make_async_copy(wf.at[span(k), pl.ds(here, half)], wave.at[k, band], s_loc.at[4])
         for k in range(chunks)
     ]
     send_p = [
         remote(
             pj.at[:, pl.ds(pl.multiple_of(there + i * piece, LANES), piece)],
-            proj.at[1, :, pl.ds(i * piece, piece)], s_p.at[i], to_m,
+            proj.at[1, :, pl.ds(i * piece, piece)], 0, s_p.at[i], to_m,
         )
         for i in range(PIECES)
     ]
     send_wm = [
-        remote(wf.at[span(k), pl.ds(there, half)], wave.at[k, band], s_wm.at[k], to_m)
+        remote(wf.at[span(k), pl.ds(there, half)], wave.at[k, band], 1, s_wm.at[k], to_m)
         for k in range(chunks)
     ]
     send_wo = [
-        remote(wf.at[span(k), pl.ds(here, half)], wave.at[k, band], s_wo.at[k], to_o)
+        remote(
+            wf.at[span(k), pl.ds(here, half)], wave.at[k, band], 2,
+            s_wo.at[max(k - EARLY + 1, 0)], to_o,
+        )
         for k in range(chunks)
     ]
     send_wf = [
-        remote(wave.at[k, m_nbr], wave.at[k, m_nbr], s_wf.at[k], to_o) for k in range(chunks)
-    ]
-    send_m = [remote(msend.at[k], mrecv.at[k], s_m.at[k], to_m) for k in range(chunks)]
-    send_d = [remote(dsend.at[k], drecv.at[k], s_d.at[k], to_twin) for k in range(chunks)]
+        remote(
+            wave.at[k, m_nbr], wave.at[k, m_nbr], 3, s_wo.at[max(k - EARLY + 1, 0)], to_o
+        )
+        for k in range(chunks)
+    ]
+    send_m = [remote(msend.at[k], mrecv.at[k], 4, s_m.at[k], to_m) for k in range(chunks)]
+    send_d = [remote(dsend.at[k], drecv.at[k], 5, s_d.at[k], to_twin) for k in range(chunks)]
     send_b = [
-        remote(mixed.at[k, z, :, :count], mixed.at[k, z, :, count:], s_b.at[k], to_m)
+        remote(mixed.at[k, z, :, :count], mixed.at[k, z, :, count:], 6, s_b.at[k], to_m)
         for k in range(chunks)
     ]
 
     def send_z(k, step):
-        return remote(
-            csend.at[k, peer(step)], parts.at[k, step], s_z.at[k, step], to_peer(step)
-        )
+        return remote(csend.at[k, peer(step)], parts.at[k, step], 7, s_z.at[k], to_peer(step))
 
     def send_e(k, step):
-        place = mixed.at[k, z, :, :count]
-        return remote(place, place, s_e.at[k, step], to_peer(step))
+        block = mixed.at[k, z, :, :count]
+        return remote(block, block, 8, s_e.at[k], to_peer(step))
 
     def send_g(k, step):
-        place = mixed.at[k, z, :, count:]
-        return remote(place, place, s_g.at[k, step], to_peer(step))
+        block = mixed.at[k, z, :, count:]
+        return remote(block, block, 8, s_e.at[k], to_peer(step))
 
     def send_n(k, t, side):
-        return remote(nsend.at[k, t, side], nrecv.at[k, t, side], s_n.at[k, t, side], to_o)
+        if side:
+            received = s_far.at[k, t]
+        else:
+            received = s_near.at[k + t if k == chunks - 1 else k]
+        return remote(nsend.at[k, t, side], nrecv.at[k, t, side], 9 + side, received, to_o)
 
     def place(k, t):
         return out.at[span(k), pl.ds(pl.multiple_of(here + t * width, LANES), width)]
 
     def send_o(k, t):
-        return remote(nfull.at[k, t], place(k, t), s_o.at[k, t], to_m)
+        return remote(nfull.at[k, t], place(k, t), 11, s_out.at[0], to_m)
 
     def write(k, t):
-        return pltpu.make_async_copy(ready.at[k, t], place(k, t), s_w.at[k, t])
+        return pltpu.make_async_copy(ready.at[k, t], place(k, t), s_out.at[1])
+
+    def arrived(ref, semaphore):
+        pltpu.make_async_copy(ref, ref, semaphore).wait()
 
     def each_peer(body):
         def step(i, carry):
@@ -259,9 +270,7 @@
         place = k
         if k >= EARLY:
             place = 0
-            local_w[k].wait()
-            send_wo[k].wait_recv()
-            send_wf[k].wait_recv()
+            arrived(wave.at[k, pl.ds(0, 2)], s_wo.at[k - EARLY + 1])
             acc[0] = jnp.zeros_like(acc[0])
 
             def tile(t):
@@ -274,7 +283,7 @@
         keep[k] = acc[place, z]
 
     def reduce(k):
-        each_peer(lambda step: send_z(k, step).wait_recv())
+        arrived(parts.at[k], s_z.at[k])
         total = keep[k]
         for step in range(zn - 1):
             total = total + parts[k, step].astype(jnp.float32)
@@ -304,8 +313,7 @@
         each_peer(lambda step: send_g(k, step).start())
 
     def expand(k):
-        each_peer(lambda step: send_e(k, step).wait_recv())
-        each_peer(lambda step: send_g(k, step).wait_recv())
+        arrived(parts.at[k], s_e.at[k])
 
         def tile(t):
             cols = columns(t)
@@ -325,17 +333,21 @@
         each_tile(lambda t: send_n(k, t, 0).start())
 
     def complete(k, t, side, owner):
-        send_n(k, t, side).wait_recv()
         cols = columns(t)
         kinetic = kin[:, cols] * wave[k, owner, :, cols].astype(jnp.float32)
         total = own[k, t, side] + nrecv[k, t, side].astype(jnp.float32)
         return (kinetic + total).astype(jnp.bfloat16)
 
     def far(k, t):
+        send_n(k, t, 1).wait_recv()
         nfull[k, t] = complete(k, t, 1, m_nbr)
         send_o(k, t).start()
 
     def near(k, t):
+        if k == chunks - 1:
+            send_n(k, t, 0).wait_recv()
+        elif t == 0:
+            arrived(nrecv.at[k, :, 0], s_near.at[k])
         ready[k, t] = complete(k, t, 0, band)
         write(k, t).start()
 
@@ -371,10 +383,8 @@
             forward(k)
         local_k.wait()
         local_p.wait()
-        for k in range(EARLY):
-            local_w[k].wait()
-            send_wo[k].wait_recv()
-            send_wf[k].wait_recv()
+        arrived(wave.at[:, 0], s_loc.at[4])
+        arrived(wave.at[pl.ds(0, EARLY), pl.ds(0, 2)], s_wo.at[0])
         acc[...] = jnp.zeros_like(acc)
         each_tile(lambda t: add_product(slice(0, EARLY), 0, columns(t)))
     for i in range(PIECES):
@@ -383,16 +393,11 @@
             add_product(slice(0, EARLY), 1, slice(i * piece, (i + 1) * piece))
 
     def settle(k):
-        for copy in send_p:
-            copy.wait_send()
-        for i in range(chunks):
-            for copy in (send_wm[i], send_wo[i], send_wf[i], send_m[i], send_d[i], send_b[i]):
-                copy.wait_send()
-            for send in (send_z, send_e, send_g):
-                each_peer(lambda step: send(i, step).wait_send())
-        for i in range(chunks - 1):
-            each_tile(lambda t: send_n(i, t, 0).wait_send())
-            each_tile(lambda t: send_n(i, t, 1).wait_send())
+        sent = (
+            proj.at[1], wave.at[:, 0], wave.at[:, 0], wave.at[:, 0], mrecv, drecv, msend, parts, parts
+        )
+        for kind, ref in enumerate(sent):
+            arrived(ref, s_send.at[kind])
 
     stages = {
         "forward": forward, "correlate": correlate, "reduce": reduce, "join": join, "mix": mix,
@@ -407,14 +412,12 @@
             else:
                 stages[stage](k)
     with jax.named_scope("others"):
-        for k in range(chunks - 1):
-            each_tile(lambda t: send_o(k, t).wait())
-        for k in range(chunks):
-            each_tile(lambda t: write(k, t).wait())
-    for side in range(2):
-        each_tile(lambda t: send_n(chunks - 1, t, side).wait_send())
+        arrived(ready, s_out.at[1])
+        arrived(nsend.at[:, :, 0], s_send.at[9])
+        arrived(nsend.at[:, :, 1], s_send.at[10])
+        arrived(nfull, s_send.at[11])
     with jax.named_scope("last"):
-        each_tile(lambda t: send_o(chunks - 1, t).wait())
+        arrived(nfull, s_out.at[0])
 
 
 def square(nga, wavefunctions, projectors, kinetic_diag, species_index, coupling):
@@ -453,20 +456,19 @@
             pltpu.VMEM((1, atoms), jnp.int32),
             pltpu.VMEM(coupling.shape, f32),
             pltpu.VMEM((count // LANES, LANES, LANES), f32),
-            dma((4 + CHUNKS,)),
-            dma((PIECES, 2)),
-            dma((CHUNKS, 2)),
-            dma((CHUNKS, 2)),
-            dma((CHUNKS, 2)),
-            dma((CHUNKS, zn - 1, 2)),
-            dma((CHUNKS, 2)),
-            dma((CHUNKS, 2)),
-            dma((CHUNKS, 2)),
-            dma((CHUNKS, zn - 1, 2)),
-            dma((CHUNKS, zn - 1, 2)),
-            dma((CHUNKS, TILES, 2, 2)),
-            dma((CHUNKS, TILES, 2)),
+            dma((12,)),
+            dma((5,)),
+            dma((PIECES,)),
+            dma((CHUNKS,)),
+            dma((CHUNKS - EARLY + 1,)),
+            dma((CHUNKS,)),
+            dma((CHUNKS,)),
+            dma((CHUNKS,)),
+            dma((CHUNKS,)),
+            dma((CHUNKS,)),
             dma((CHUNKS, TILES)),
+            dma((CHUNKS + TILES - 1,)),
+            dma((2,)),
         ],
         compiler_params=pltpu.CompilerParams(
             collective_id=0, has_side_effects=True, vmem_limit_bytes=50 * 2**20

time: 186 us -> 185 us (level)
  Pallas kernels: 181 us -> 179 us
    pallas_call x1, Pallas kernels: 181 us -> 179 us  [square(): pl.pallas_call(functools.partial(kernel, nga), out_shape=jax.ShapeDtypeSt...]
where the time goes in v3:
time: 185 us; the launch traced here: 183 us
  Pallas kernels  179 us (97%)
  local copies, waits for them, and re-layouts  3.86 us (2%)
    pallas_call x1, Pallas kernels, square(): pl.pallas_call(functools.partial(kernel, nga), out_shape=jax.ShapeDtypeSt...  179 us
    unnamed x7, local copies, waits for them, and re-layouts  3.86 us

profile of v3, /device:TPU:28, one launch (start us, length us, event | category | flops | bytes accessed | tf_op | source)
XLA Modules:
  0.0 182.8 jit_solution(11104051951461055617)
XLA Ops:
  0.0 0.0 copy-start
  0.0 0.8 copy-done
  0.8 0.0 copy-start.1
  0.8 0.7 copy-done.1
  1.5 0.0 copy-start.2
  1.5 0.7 copy-done.2
  2.2 178.9 %shard_map.55 = bf16[128,12288]{1,0:T(8,128)(2,1)S(1)} custom-call(bf16[128,12288]{1,0:T(8,128)(2,1)} %wf.1, bf16[512,12288]{1,0:T(8,128)(2,1)} %pj.1, f32[1,12288]{1,0:T(1,128)S(1)} %bitcast.2, s32[1,256]{1,0:T(1,128)S(1)} %bitcast.3, f32[4,8,8]{2,1,0:T(8,128)S(1)} %copy-done.1), custom_call_target="tpu_custom_call" | custom-call | tf_op jit(solution)/shard_map/pallas_call | solution.py:433
  181.1 1.7 copy.7
Async XLA Ops:
  0.0 0.8 copy-start
  0.8 0.7 copy-start.1
  1.5 0.7 copy-start.2

commit v4 on v3

--- a/solution.py
+++ b/solution.py
@@ -63,13 +63,13 @@
 
 def schedule():
     times = {
-        "correlate": (0.3, 0.5, 16.5, 24.6),
+        "correlate": (0.3, 0.5, 16.6, 24.8),
         "forward": (None, None, 4.0, 9.5),
-        "reduce": (7.5, 12.0, 29.3, 37.4),
-        "join": (9.7, 15.0, 32.2, 40.0),
-        "mix": (11.3, 21.2, 33.4, 41.2),
-        "share": (14.4, 24.0, 36.0, 44.0),
-        "expand": (21.5, 29.6, 42.0, 50.0),
+        "reduce": (7.5, 12.0, 29.7, 38.0),
+        "join": (9.7, 15.0, 30.0, 39.5),
+        "mix": (11.3, 16.3, 31.2, 40.7),
+        "share": (14.4, 22.1, 36.1, 43.2),
+        "expand": (22.2, 31.3, 43.5, 50.0),
         "settle": (57.0, None, None, None),
     }
     events = [
@@ -78,9 +78,9 @@
         for k, at in enumerate(row)
         if at is not None
     ]
-    for k, (first, step) in enumerate(((29.5, 0.02), (36.5, 1.2), (50.5, 1.2), (62.0, 1.0))):
-        events += [(first + step * t, "far", k, t) for t in range(TILES)]
-    for k, first in enumerate((44.2, 52.6, 58.0, 70.0)):
+    for k, row in enumerate(((29.8, 29.82, 36.02, 36.04), (40.9, 40.92, 46.0, 46.1), (50.5, 51.5, 52.5, 53.5), (62.0, 63.0, 64.0, 65.0))):
+        events += [(at, "far", k, t) for t, at in enumerate(row)]
+    for k, first in enumerate((46.5, 52.6, 58.0, 70.0)):
         events += [(first + 0.05 * t, "near", k, t) for t in range(TILES)]
     return [event[1:] for event in sorted(events)]
 
@@ -89,7 +89,7 @@
     nga, wf, pj, kin_hbm, species_hbm, coupling_hbm, out,
     proj, wave, acc, csend, keep, parts, msend, mrecv, dsend, drecv, mixed,
     nsend, nrecv, own, nfull, ready, kin, species, coupling, tiles,
-    s_send, s_loc, s_p, s_wm, s_wo, s_m, s_d, s_b, s_z, s_e, s_far, s_near, s_out,
+    s_send, s_loc, s_p, s_wm, s_wo, s_m, s_d, s_b, s_z, s_e, s_far, s_near, s_out, s_token,
 ):
     chunks, _, rows, half = wave.shape
     _, zn, share, both = csend.shape
@@ -125,9 +125,9 @@
     local_p = pltpu.make_async_copy(pj.at[:, pl.ds(here, half)], proj.at[0], s_loc.at[0])
     local_k = pltpu.make_async_copy(kin_hbm.at[:, pl.ds(here, half)], kin, s_loc.at[1])
     local_s = pltpu.make_async_copy(species_hbm, species, s_loc.at[2])
-    local_c = pltpu.make_async_copy(coupling_hbm, coupling, s_loc.at[3])
+    local_c = pltpu.make_async_copy(coupling_hbm, coupling, s_loc.at[4])
     local_w = [
-        pltpu.make_async_copy(wf.at[span(k), pl.ds(here, half)], wave.at[k, band], s_loc.at[4])
+        pltpu.make_async_copy(wf.at[span(k), pl.ds(here, half)], wave.at[k, band], s_loc.at[3])
         for k in range(chunks)
     ]
     send_p = [
@@ -172,18 +172,18 @@
         block = mixed.at[k, z, :, count:]
         return remote(block, block, 8, s_e.at[k], to_peer(step))
 
+    def send_near(k):
+        return remote(nsend.at[k, 0], nrecv.at[k, 0], 9, s_near.at[k], to_o)
+
     def send_n(k, t, side):
-        if side:
-            received = s_far.at[k, t]
-        else:
-            received = s_near.at[k + t if k == chunks - 1 else k]
-        return remote(nsend.at[k, t, side], nrecv.at[k, t, side], 9 + side, received, to_o)
+        received = s_far.at[k, t] if side else s_near.at[k + t]
+        return remote(nsend.at[k, side, t], nrecv.at[k, side, t], 9, received, to_o)
 
     def place(k, t):
         return out.at[span(k), pl.ds(pl.multiple_of(here + t * width, LANES), width)]
 
     def send_o(k, t):
-        return remote(nfull.at[k, t], place(k, t), 11, s_out.at[0], to_m)
+        return remote(nfull.at[k, t], place(k, t), 10, s_out.at[0], to_m)
 
     def write(k, t):
         return pltpu.make_async_copy(ready.at[k, t], place(k, t), s_out.at[1])
@@ -325,17 +325,20 @@
                 jnp.concatenate(picks, axis=0), proj[:, :, cols].reshape(both, width),
                 preferred_element_type=jnp.float32,
             ).reshape(4, rows, width)
-            nsend[k, t] = value[:2].astype(jnp.bfloat16)
+            nsend[k, :, t] = value[:2].astype(jnp.bfloat16)
             send_n(k, t, 1).start()
             own[k, t] = value[2:]
 
         each_tile(tile)
-        each_tile(lambda t: send_n(k, t, 0).start())
+        if k == chunks - 1:
+            each_tile(lambda t: send_n(k, t, 0).start())
+        else:
+            send_near(k).start()
 
     def complete(k, t, side, owner):
         cols = columns(t)
         kinetic = kin[:, cols] * wave[k, owner, :, cols].astype(jnp.float32)
-        total = own[k, t, side] + nrecv[k, t, side].astype(jnp.float32)
+        total = own[k, t, side] + nrecv[k, side, t].astype(jnp.float32)
         return (kinetic + total).astype(jnp.bfloat16)
 
     def far(k, t):
@@ -347,27 +350,30 @@
         if k == chunks - 1:
             send_n(k, t, 0).wait_recv()
         elif t == 0:
-            arrived(nrecv.at[k, :, 0], s_near.at[k])
+            send_near(k).wait_recv()
         ready[k, t] = complete(k, t, 0, band)
         write(k, t).start()
 
     barrier = pltpu.get_barrier_semaphore()
+
+    def greet(semaphore, device):
+        pl.semaphore_signal(
+            semaphore, inc=1, device_id=device, device_id_type=pl.DeviceIdType.MESH
+        )
+
+    above, below = {"ga": (z + 1) * 2 + core}, {"ga": (z - 1) * 2 + core}
+    has_above, has_below = z < zn - 1, z > 0
     for device in (to_m, to_o, to_twin):
-        pl.semaphore_signal(
-            barrier, inc=1, device_id=device, device_id_type=pl.DeviceIdType.MESH
-        )
-    each_peer(
-        lambda step: pl.semaphore_signal(
-            barrier, inc=1, device_id=to_peer(step), device_id_type=pl.DeviceIdType.MESH
-        )
-    )
+        greet(barrier, device)
+    pl.when(has_above)(lambda: greet(barrier, above))
+    pl.when(has_below)(lambda: greet(barrier, below))
     local_p.start()
     for copy in local_w:
         copy.start()
     local_s.start()
     local_c.start()
     local_k.start()
-    pl.semaphore_wait(barrier, zn + 2)
+    pl.semaphore_wait(barrier, 3 + has_above.astype(jnp.int32) + has_below.astype(jnp.int32))
 
     for k in range(EARLY):
         send_wm[k].start()
@@ -376,6 +382,11 @@
         copy.start()
     for k in range(EARLY, chunks):
         send_wm[k].start()
+    with jax.named_scope("tokens"):
+        pl.when(has_below)(lambda: pl.semaphore_wait(s_token.at[0], 1))
+        pl.when(has_above)(lambda: greet(s_token.at[0], above))
+        pl.when(has_above)(lambda: pl.semaphore_wait(s_token.at[1], 1))
+        pl.when(has_below)(lambda: greet(s_token.at[1], below))
     with jax.named_scope("build"):
         build_tiles()
     with jax.named_scope("first"):
@@ -383,7 +394,7 @@
             forward(k)
         local_k.wait()
         local_p.wait()
-        arrived(wave.at[:, 0], s_loc.at[4])
+        arrived(wave.at[:, 0], s_loc.at[3])
         arrived(wave.at[pl.ds(0, EARLY), pl.ds(0, 2)], s_wo.at[0])
         acc[...] = jnp.zeros_like(acc)
         each_tile(lambda t: add_product(slice(0, EARLY), 0, columns(t)))
@@ -413,9 +424,8 @@
                 stages[stage](k)
     with jax.named_scope("others"):
         arrived(ready, s_out.at[1])
-        arrived(nsend.at[:, :, 0], s_send.at[9])
-        arrived(nsend.at[:, :, 1], s_send.at[10])
-        arrived(nfull, s_send.at[11])
+        arrived(nsend, s_send.at[9])
+        arrived(nfull, s_send.at[10])
     with jax.named_scope("last"):
         arrived(nfull, s_out.at[0])
 
@@ -447,8 +457,8 @@
             pltpu.VMEM((CHUNKS, share, count), f32),
             pltpu.VMEM((CHUNKS, share, count), f32),
             pltpu.VMEM((CHUNKS, zn, share, 2 * count), bf16),
-            pltpu.VMEM((CHUNKS, TILES, 2, rows, width), bf16),
-            pltpu.VMEM((CHUNKS, TILES, 2, rows, width), bf16),
+            pltpu.VMEM((CHUNKS, 2, TILES, rows, width), bf16),
+            pltpu.VMEM((CHUNKS, 2, TILES, rows, width), bf16),
             pltpu.VMEM((CHUNKS, TILES, 2, rows, width), f32),
             pltpu.VMEM((CHUNKS, TILES, rows, width), bf16),
             pltpu.VMEM((CHUNKS, TILES, rows, width), bf16),
@@ -456,7 +466,7 @@
             pltpu.VMEM((1, atoms), jnp.int32),
             pltpu.VMEM(coupling.shape, f32),
             pltpu.VMEM((count // LANES, LANES, LANES), f32),
-            dma((12,)),
+            dma((11,)),
             dma((5,)),
             dma((PIECES,)),
             dma((CHUNKS,)),
@@ -469,6 +479,7 @@
             dma((CHUNKS, TILES)),
             dma((CHUNKS + TILES - 1,)),
             dma((2,)),
+            pltpu.SemaphoreType.REGULAR((2,)),
         ],
         compiler_params=pltpu.CompilerParams(
             collective_id=0, has_side_effects=True, vmem_limit_bytes=50 * 2**20

time: 185 us -> 184 us (level)
  no operation moved by 1% of the time
where the time goes in v4:
time: 184 us
  Pallas kernels  180 us (98%)
  local copies, waits for them, and re-layouts  3.86 us (2%)
    pallas_call x1, Pallas kernels, square(): pl.pallas_call(functools.partial(kernel, nga), out_shape=jax.ShapeDtypeSt...  180 us
    unnamed x7, local copies, waits for them, and re-layouts  3.86 us

profile of v4, /device:TPU:28, one launch (start us, length us, event | category | flops | bytes accessed | tf_op | source)
XLA Modules:
  0.0 183.6 jit_solution(8266746809328015577)
XLA Ops:
  0.0 0.0 copy-start
  0.0 0.8 copy-done
  0.8 0.0 copy-start.1
  0.8 0.7 copy-done.1
  1.5 0.0 copy-start.2
  1.5 0.7 copy-done.2
  2.2 179.7 %shard_map.55 = bf16[128,12288]{1,0:T(8,128)(2,1)S(1)} custom-call(bf16[128,12288]{1,0:T(8,128)(2,1)} %wf.1, bf16[512,12288]{1,0:T(8,128)(2,1)} %pj.1, f32[1,12288]{1,0:T(1,128)S(1)} %bitcast.2, s32[1,256]{1,0:T(1,128)S(1)} %bitcast.3, f32[4,8,8]{2,1,0:T(8,128)S(1)} %copy-done.1), custom_call_target="tpu_custom_call" | custom-call | tf_op jit(solution)/shard_map/pallas_call | solution.py:443
  181.9 1.7 copy.7
Async XLA Ops:
  0.0 0.8 copy-start
  0.8 0.7 copy-start.1
  1.5 0.7 copy-start.2

commit v5 on v4

--- a/solution.py
+++ b/solution.py
@@ -428,6 +428,10 @@
         arrived(nfull, s_send.at[10])
     with jax.named_scope("last"):
         arrived(nfull, s_out.at[0])
+
+
+def in_hbm(array):
+    return pltpu.with_memory_space_constraint(array, pltpu.HBM)
 
 
 def square(nga, wavefunctions, projectors, kinetic_diag, species_index, coupling):
@@ -485,8 +489,8 @@
             collective_id=0, has_side_effects=True, vmem_limit_bytes=50 * 2**20
         ),
     )(
-        wavefunctions, projectors, kinetic_diag.reshape(1, waves),
-        species_index.reshape(1, atoms), coupling,
+        wavefunctions, projectors, in_hbm(kinetic_diag.reshape(1, waves)),
+        in_hbm(species_index.reshape(1, atoms)), in_hbm(coupling),
     )
 
 

time: 184 us -> 182 us (0.989)
  local copies, waits for them, and re-layouts: 3.86 us -> 1.67 us
    unnamed x7 -> x1, local copies, waits for them, and re-layouts: 3.86 us -> 1.67 us
where the time goes in v5:
time: 182 us; the launch traced here: 181 us
  Pallas kernels  180 us (99%)
    pallas_call x1, Pallas kernels, square(): pl.pallas_call(functools.partial(kernel, nga), out_shape=jax.ShapeDtypeSt...  180 us

profile of v5, /device:TPU:28, one launch (start us, length us, event | category | flops | bytes accessed | tf_op | source)
XLA Modules:
  0.0 181.4 jit_solution(1918276884000739787)
XLA Ops:
  0.0 179.7 %shard_map.55 = bf16[128,12288]{1,0:T(8,128)(2,1)S(1)} custom-call(bf16[128,12288]{1,0:T(8,128)(2,1)} %wf.1, bf16[512,12288]{1,0:T(8,128)(2,1)} %pj.1, f32[1,12288]{1,0:T(1,128)} %bitcast.2, s32[1,256]{1,0:T(1,128)} %bitcast.3, f32[4,8,8]{2,1,0:T(8,128)} %coupling_hbm.1), custom_call_target="tpu_custom_call" | custom-call | tf_op jit(solution)/shard_map/pallas_call | solution.py:447
  179.7 1.7 copy.7

commit v6 on v5

--- a/solution.py
+++ b/solution.py
@@ -65,11 +65,12 @@
     times = {
         "correlate": (0.3, 0.5, 16.6, 24.8),
         "forward": (None, None, 4.0, 9.5),
-        "reduce": (7.5, 12.0, 29.7, 38.0),
-        "join": (9.7, 15.0, 30.0, 39.5),
-        "mix": (11.3, 16.3, 31.2, 40.7),
-        "share": (14.4, 22.1, 36.1, 43.2),
-        "expand": (22.2, 31.3, 43.5, 50.0),
+        "reduce": (7.5, 12.0, 29.7, 36.5),
+        "join": (9.7, 15.0, 30.0, 38.0),
+        "mix": (11.3, 16.3, 31.2, 39.2),
+        "share": (14.4, 22.1, 36.1, 42.2),
+        "expand": (22.2, 31.3, 42.0, 50.0),
+        "turn": (1.0, None, None, None),
         "settle": (57.0, None, None, None),
     }
     events = [
@@ -78,7 +79,7 @@
         for k, at in enumerate(row)
         if at is not None
     ]
-    for k, row in enumerate(((29.8, 29.82, 36.02, 36.04), (40.9, 40.92, 46.0, 46.1), (50.5, 51.5, 52.5, 53.5), (62.0, 63.0, 64.0, 65.0))):
+    for k, row in enumerate(((29.8, 29.81, 29.82, 29.83), (39.6, 39.7, 39.8, 39.9), (50.5, 51.5, 52.5, 53.5), (62.0, 63.0, 64.0, 65.0))):
         events += [(at, "far", k, t) for t, at in enumerate(row)]
     for k, first in enumerate((46.5, 52.6, 58.0, 70.0)):
         events += [(first + 0.05 * t, "near", k, t) for t in range(TILES)]
@@ -87,8 +88,8 @@
 
 def kernel(
     nga, wf, pj, kin_hbm, species_hbm, coupling_hbm, out,
-    proj, wave, acc, csend, keep, parts, msend, mrecv, dsend, drecv, mixed,
-    nsend, nrecv, own, nfull, ready, kin, species, coupling, tiles,
+    proj, flip, wave, acc, csend, keep, parts, msend, mrecv, dsend, drecv, mixed,
+    nsend, nrecv, own, nfull, kin, species, coupling, tiles,
     s_send, s_loc, s_p, s_wm, s_wo, s_m, s_d, s_b, s_z, s_e, s_far, s_near, s_out, s_token,
 ):
     chunks, _, rows, half = wave.shape
@@ -185,9 +186,6 @@
     def send_o(k, t):
         return remote(nfull.at[k, t], place(k, t), 10, s_out.at[0], to_m)
 
-    def write(k, t):
-        return pltpu.make_async_copy(ready.at[k, t], place(k, t), s_out.at[1])
-
     def arrived(ref, semaphore):
         pltpu.make_async_copy(ref, ref, semaphore).wait()
 
@@ -217,6 +215,14 @@
         )
         product = product.reshape(-1, zn, share, count)
         acc[: product.shape[0], :, :, slot * count : (slot + 1) * count] += product
+
+    def turn(slot, i):
+        part = pl.ds(pl.multiple_of(i * piece, LANES), piece)
+        flip[part, slot * count : (slot + 1) * count] = proj[slot, :, part].T
+
+    def turn_own(i, carry):
+        turn(0, i)
+        return carry
 
     def build_tiles():
         kinds, npa = coupling.shape[0], coupling.shape[1]
@@ -274,8 +280,11 @@
             acc[0] = jnp.zeros_like(acc[0])
 
             def tile(t):
-                add_product(slice(k, k + 1), 0, columns(t))
-                add_product(slice(k, k + 1), 1, columns(t))
+                product = jnp.dot(
+                    wave[k, :, :, columns(t)].reshape(4 * rows, width), flip[columns(t), :],
+                    preferred_element_type=jnp.float32,
+                )
+                acc[0] += product.reshape(zn, share, both)
 
             each_tile(tile)
         csend[k] = acc[place].astype(jnp.bfloat16)
@@ -327,7 +336,7 @@
             ).reshape(4, rows, width)
             nsend[k, :, t] = value[:2].astype(jnp.bfloat16)
             send_n(k, t, 1).start()
-            own[k, t] = value[2:]
+            own[k % 3, t] = value[2:]
 
         each_tile(tile)
         if k == chunks - 1:
@@ -338,7 +347,7 @@
     def complete(k, t, side, owner):
         cols = columns(t)
         kinetic = kin[:, cols] * wave[k, owner, :, cols].astype(jnp.float32)
-        total = own[k, t, side] + nrecv[k, side, t].astype(jnp.float32)
+        total = own[k % 3, t, side] + nrecv[k, side, t].astype(jnp.float32)
         return (kinetic + total).astype(jnp.bfloat16)
 
     def far(k, t):
@@ -351,8 +360,9 @@
             send_n(k, t, 0).wait_recv()
         elif t == 0:
             send_near(k).wait_recv()
-        ready[k, t] = complete(k, t, 0, band)
-        write(k, t).start()
+        out[span(k), pl.ds(pl.multiple_of(here + t * width, LANES), width)] = complete(
+            k, t, 0, band
+        )
 
     barrier = pltpu.get_barrier_semaphore()
 
@@ -398,10 +408,13 @@
         arrived(wave.at[pl.ds(0, EARLY), pl.ds(0, 2)], s_wo.at[0])
         acc[...] = jnp.zeros_like(acc)
         each_tile(lambda t: add_product(slice(0, EARLY), 0, columns(t)))
+        lax.fori_loop(0, PIECES, turn_own, 0)
     for i in range(PIECES):
         with jax.named_scope(f"piece#i={i}"):
             send_p[i].wait_recv()
             add_product(slice(0, EARLY), 1, slice(i * piece, (i + 1) * piece))
+            if i < PIECES - 1:
+                turn(1, i)
 
     def settle(k):
         sent = (
@@ -414,6 +427,10 @@
         "forward": forward, "correlate": correlate, "reduce": reduce, "join": join, "mix": mix,
         "share": share_out, "expand": expand, "settle": settle,
     }
+    def turn_last(k):
+        turn(1, PIECES - 1)
+
+    stages["turn"] = turn_last
     for stage, k, t in schedule():
         with jax.named_scope(f"{stage}#k={k}#t={t}"):
             if stage == "far":
@@ -423,7 +440,6 @@
             else:
                 stages[stage](k)
     with jax.named_scope("others"):
-        arrived(ready, s_out.at[1])
         arrived(nsend, s_send.at[9])
         arrived(nfull, s_send.at[10])
     with jax.named_scope("last"):
@@ -448,9 +464,10 @@
         functools.partial(kernel, nga),
         out_shape=jax.ShapeDtypeStruct((bands, waves), bf16),
         in_specs=[anywhere] * 5,
-        out_specs=anywhere,
+        out_specs=pl.BlockSpec(memory_space=pltpu.VMEM),
         scratch_shapes=[
             pltpu.VMEM((2, count, half), bf16),
+            pltpu.VMEM((half, 2 * count), bf16),
             pltpu.VMEM((CHUNKS, 4, rows, half), bf16),
             pltpu.VMEM((EARLY, zn, share, 2 * count), f32),
             pltpu.VMEM((CHUNKS, zn, share, 2 * count), bf16),
@@ -463,8 +480,7 @@
             pltpu.VMEM((CHUNKS, zn, share, 2 * count), bf16),
             pltpu.VMEM((CHUNKS, 2, TILES, rows, width), bf16),
             pltpu.VMEM((CHUNKS, 2, TILES, rows, width), bf16),
-            pltpu.VMEM((CHUNKS, TILES, 2, rows, width), f32),
-            pltpu.VMEM((CHUNKS, TILES, rows, width), bf16),
+            pltpu.VMEM((3, TILES, 2, rows, width), f32),
             pltpu.VMEM((CHUNKS, TILES, rows, width), bf16),
             pltpu.VMEM((1, half), f32),
             pltpu.VMEM((1, atoms), jnp.int32),
@@ -482,11 +498,11 @@
             dma((CHUNKS,)),
             dma((CHUNKS, TILES)),
             dma((CHUNKS + TILES - 1,)),
-            dma((2,)),
+            dma((1,)),
             pltpu.SemaphoreType.REGULAR((2,)),
         ],
         compiler_params=pltpu.CompilerParams(
-            collective_id=0, has_side_effects=True, vmem_limit_bytes=50 * 2**20
+            collective_id=0, has_side_effects=True, vmem_limit_bytes=53_300_000
         ),
     )(
         wavefunctions, projectors, in_hbm(kinetic_diag.reshape(1, waves)),

time: 182 us -> 181 us (level)
  no operation moved by 1% of the time
where the time goes in v6:
time: 181 us
  Pallas kernels  179 us (99%)
    pallas_call x1, Pallas kernels, square(): pl.pallas_call(functools.partial(kernel, nga), out_shape=jax.ShapeDtypeSt...  179 us

profile of v6, /device:TPU:28, one launch (start us, length us, event | category | flops | bytes accessed | tf_op | source)
XLA Modules:
  0.0 180.5 jit_solution(1383230248350379139)
XLA Ops:
  0.0 178.9 %shard_map.55 = bf16[128,12288]{1,0:T(8,128)(2,1)S(1)} custom-call(bf16[128,12288]{1,0:T(8,128)(2,1)} %wf.1, bf16[512,12288]{1,0:T(8,128)(2,1)} %pj.1, f32[1,12288]{1,0:T(1,128)} %bitcast.2, s32[1,256]{1,0:T(1,128)} %bitcast.3, f32[4,8,8]{2,1,0:T(8,128)} %coupling_hbm.1), custom_call_target="tpu_custom_call" | custom-call | tf_op jit(solution)/shard_map/pallas_call | solution.py:463
  178.9 1.7 copy.7

commit v7 on v6

--- a/solution.py
+++ b/solution.py
@@ -144,47 +144,47 @@
     ]
     send_wo = [
         remote(
-            wf.at[span(k), pl.ds(here, half)], wave.at[k, band], 2,
+            wf.at[span(k), pl.ds(here, half)], wave.at[k, band], 1,
             s_wo.at[max(k - EARLY + 1, 0)], to_o,
         )
         for k in range(chunks)
     ]
     send_wf = [
         remote(
-            wave.at[k, m_nbr], wave.at[k, m_nbr], 3, s_wo.at[max(k - EARLY + 1, 0)], to_o
+            wave.at[k, m_nbr], wave.at[k, m_nbr], 1, s_wo.at[max(k - EARLY + 1, 0)], to_o
         )
         for k in range(chunks)
     ]
     send_m = [remote(msend.at[k], mrecv.at[k], 4, s_m.at[k], to_m) for k in range(chunks)]
-    send_d = [remote(dsend.at[k], drecv.at[k], 5, s_d.at[k], to_twin) for k in range(chunks)]
+    send_d = [remote(dsend.at[k], drecv.at[k], 2, s_d.at[k], to_twin) for k in range(chunks)]
     send_b = [
-        remote(mixed.at[k, z, :, :count], mixed.at[k, z, :, count:], 6, s_b.at[k], to_m)
+        remote(mixed.at[k, z, :, :count], mixed.at[k, z, :, count:], 4, s_b.at[k], to_m)
         for k in range(chunks)
     ]
 
     def send_z(k, step):
-        return remote(csend.at[k, peer(step)], parts.at[k, step], 7, s_z.at[k], to_peer(step))
+        return remote(csend.at[k, peer(step)], parts.at[k, step], 3, s_z.at[k], to_peer(step))
 
     def send_e(k, step):
         block = mixed.at[k, z, :, :count]
-        return remote(block, block, 8, s_e.at[k], to_peer(step))
+        return remote(block, block, 5, s_e.at[k], to_peer(step))
 
     def send_g(k, step):
         block = mixed.at[k, z, :, count:]
-        return remote(block, block, 8, s_e.at[k], to_peer(step))
+        return remote(block, block, 5, s_e.at[k], to_peer(step))
 
     def send_near(k):
-        return remote(nsend.at[k, 0], nrecv.at[k, 0], 9, s_near.at[k], to_o)
+        return remote(nsend.at[k, 0], nrecv.at[k, 0], 6, s_near.at[k], to_o)
 
     def send_n(k, t, side):
-        received = s_far.at[k, t] if side else s_near.at[k + t]
-        return remote(nsend.at[k, side, t], nrecv.at[k, side, t], 9, received, to_o)
+        received = s_far.at[k if k < 2 else 2 + (k - 2) * TILES + t] if side else s_near.at[k + t]
+        return remote(nsend.at[k, side, t], nrecv.at[k, side, t], 6, received, to_o)
 
     def place(k, t):
         return out.at[span(k), pl.ds(pl.multiple_of(here + t * width, LANES), width)]
 
     def send_o(k, t):
-        return remote(nfull.at[k, t], place(k, t), 10, s_out.at[0], to_m)
+        return remote(nfull.at[k, t], place(k, t), 7, s_out.at[0], to_m)
 
     def arrived(ref, semaphore):
         pltpu.make_async_copy(ref, ref, semaphore).wait()
@@ -351,7 +351,10 @@
         return (kinetic + total).astype(jnp.bfloat16)
 
     def far(k, t):
-        send_n(k, t, 1).wait_recv()
+        if k >= 2:
+            send_n(k, t, 1).wait_recv()
+        elif t == 0:
+            arrived(nrecv.at[k, 1], s_far.at[k])
         nfull[k, t] = complete(k, t, 1, m_nbr)
         send_o(k, t).start()
 
@@ -417,9 +420,7 @@
                 turn(1, i)
 
     def settle(k):
-        sent = (
-            proj.at[1], wave.at[:, 0], wave.at[:, 0], wave.at[:, 0], mrecv, drecv, msend, parts, parts
-        )
+        sent = (proj.at[1], wave.at[:, pl.ds(0, 3)], drecv, parts, drecv, parts)
         for kind, ref in enumerate(sent):
             arrived(ref, s_send.at[kind])
 
@@ -440,8 +441,8 @@
             else:
                 stages[stage](k)
     with jax.named_scope("others"):
-        arrived(nsend, s_send.at[9])
-        arrived(nfull, s_send.at[10])
+        arrived(nsend, s_send.at[6])
+        arrived(nfull, s_send.at[7])
     with jax.named_scope("last"):
         arrived(nfull, s_out.at[0])
 
@@ -486,7 +487,7 @@
             pltpu.VMEM((1, atoms), jnp.int32),
             pltpu.VMEM(coupling.shape, f32),
             pltpu.VMEM((count // LANES, LANES, LANES), f32),
-            dma((11,)),
+            dma((8,)),
             dma((5,)),
             dma((PIECES,)),
             dma((CHUNKS,)),
@@ -496,7 +497,7 @@
             dma((CHUNKS,)),
             dma((CHUNKS,)),
             dma((CHUNKS,)),
-            dma((CHUNKS, TILES)),
+            dma((2 + (CHUNKS - 2) * TILES,)),
             dma((CHUNKS + TILES - 1,)),
             dma((1,)),
             pltpu.SemaphoreType.REGULAR((2,)),

time: 181 us -> 181 us (level)
  no operation moved by 1% of the time
where the time goes in v7:
time: 181 us; the launch traced here: 180 us
  Pallas kernels  179 us (99%)
    pallas_call x1, Pallas kernels, square(): pl.pallas_call(functools.partial(kernel, nga), out_shape=jax.ShapeDtypeSt...  179 us

profile of v7, /device:TPU:28, one launch (start us, length us, event | category | flops | bytes accessed | tf_op | source)
XLA Modules:
  0.0 180.5 jit_solution(13699744317511144902)
XLA Ops:
  0.0 178.8 %shard_map.55 = bf16[128,12288]{1,0:T(8,128)(2,1)S(1)} custom-call(bf16[128,12288]{1,0:T(8,128)(2,1)} %wf.1, bf16[512,12288]{1,0:T(8,128)(2,1)} %pj.1, f32[1,12288]{1,0:T(1,128)} %bitcast.2, s32[1,256]{1,0:T(1,128)} %bitcast.3, f32[4,8,8]{2,1,0:T(8,128)} %coupling_hbm.1), custom_call_target="tpu_custom_call" | custom-call | tf_op jit(solution)/shard_map/pallas_call | solution.py:464
  178.8 1.7 copy.7
